TPU v7x, 32 devices: a whole 2x2x4 slice. The times are simulated.
32 devices in a mesh: slab: 8 (over z, y), chan: 4 (over x, core).
Axes of the slice: x: 2, y: 2, z: 4, core: 2. Of those that a mesh axis runs over, the one named last changes fastest.
Arguments:
- saved_input: float32 [512, 48, 256], P('chan', 'slab'), may hold values from -6 to 6
- pre_first: float32 [512, 48, 256], P('chan', 'slab'), may hold values from -8 to 8
- pre_second: float32 [512, 48, 256], P('chan', 'slab'), may hold values from -8 to 8
- out_grad: float32 [512, 48, 256], P('chan', 'slab'), may hold values from -12 to 12
- weight_first: float32 [27, 512, 512], P(None, 'chan'), may hold values from -0.0546875 to 0.0546875
- weight_second: float32 [27, 512, 512], P(None, 'chan'), may hold values from -0.0546875 to 0.0546875
Outputs:
- input_grad: float32 [512, 48, 256], P('chan', 'slab')
- grad_weight_first: float32 [27, 512, 512], P(None, 'chan', 'slab')
- grad_weight_second: float32 [27, 512, 512], P(None, 'chan', 'slab')
All inputs are finite; a program needn't handle non-finite values.
Results may differ from a plain program's by a relative error of at most 0.00013.
Values sent between devices are 32-bit elements; how exact they have to be, the bound alone decides.
A program may use at most 320 MiB of HBM per device.

v0:
```python
import math

import jax
import jax.numpy as jnp
from jax import lax
from jax.sharding import PartitionSpec as P

STEPS = (-1, 0, 1)
IN_PLANE = [(row_step, col_step) for row_step in STEPS for col_step in STEPS]


def with_rim(value):
    count = lax.axis_size("slab")
    up = [(i, i + 1) for i in range(count - 1)]
    down = [(j, i) for i, j in up]
    before = lax.ppermute(value[-1:], "slab", up)
    after = lax.ppermute(value[:1], "slab", down)
    return jnp.concatenate([before, value, after], axis=0)


def silu_slope(values):
    sigma = jax.nn.sigmoid(values)
    return sigma * (1.0 + values * (1.0 - sigma))


def shift_cells(block, row_step, col_step, side_len):
    area_cells = block.shape[-1]
    if row_step == 0 and col_step == 0:
        return block
    cell_ids = lax.iota(jnp.int32, area_cells)
    row_ids = cell_ids // side_len
    col_ids = cell_ids % side_len
    valid = (
        (row_ids + row_step >= 0)
        & (row_ids + row_step < side_len)
        & (col_ids + col_step >= 0)
        & (col_ids + col_step < side_len)
    )
    rolled = jnp.roll(block, -(row_step * side_len + col_step), axis=-1)
    return jnp.where(valid, rolled, jnp.zeros_like(rolled))


def gather_channels(rimmed):
    planes, channels, cells = rimmed.shape
    portion = lax.all_gather(rimmed, "chan", axis=0)
    return portion.transpose(1, 0, 2, 3).reshape(planes, -1, cells)


def input_side(portion, weight, side_len):
    planes = portion.shape[0] - 2
    channels, total = weight.shape[1:]
    near = jnp.stack([portion[1 - a : 1 - a + planes] for a in STEPS], 0)
    rows = weight.reshape(len(STEPS), len(IN_PLANE) * channels, total)
    summed = lax.dot_general(
        rows,
        near,
        (((0, 2), (0, 2)), ((), ())),
        precision=lax.Precision.HIGH,
        preferred_element_type=jnp.float32,
    )
    summed = summed.reshape(len(IN_PLANE), channels, planes, -1)
    result = jnp.zeros(summed.shape[1:], jnp.float32)
    for index, (row_step, col_step) in enumerate(IN_PLANE):
        result = result + shift_cells(summed[index], -row_step, -col_step, side_len)
    return result.transpose(1, 0, 2)


def weight_side(rimmed, centre, side_len):
    planes, total, cells = centre.shape
    channels = rimmed.shape[1]
    moved = jnp.stack([shift_cells(rimmed, b, c, side_len) for b, c in IN_PLANE], 1)
    moved = moved.reshape(planes + 2, len(IN_PLANE) * channels, cells)
    voxels = planes * lax.axis_size("slab") * cells
    parts = []
    for a in STEPS:
        part = lax.dot_general(
            moved[1 + a : 1 + a + planes],
            centre,
            (((0, 2), (0, 2)), ((), ())),
            precision=lax.Precision.HIGH,
            preferred_element_type=jnp.float32,
        )
        parts.append(part.reshape(len(IN_PLANE), channels, total) / math.sqrt(voxels))
    return parts


def reduce_parts(parts):
    done = [lax.psum_scatter(part, "slab", scatter_dimension=2, tiled=True) for part in parts]
    return jnp.concatenate(done, 0)


def per_device(saved_input, pre_first, pre_second, out_grad, weight_first, weight_second):
    side_len = math.isqrt(saved_input.shape[-1])
    saved_input, pre_first, pre_second, out_grad = (
        value.transpose(1, 0, 2) for value in (saved_input, pre_first, pre_second, out_grad)
    )
    second_grad = out_grad * silu_slope(pre_second)
    second_all = gather_channels(with_rim(second_grad))
    hidden = with_rim(jax.nn.silu(pre_first))
    input_rim = with_rim(saved_input)
    hidden_grad = input_side(second_all, weight_second, side_len)
    first_grad = hidden_grad * silu_slope(pre_first)
    first_all = gather_channels(with_rim(first_grad))
    second_parts = weight_side(hidden, second_all[1:-1], side_len)
    first_all, second_parts = lax.optimization_barrier((first_all, second_parts))
    first_parts = weight_side(input_rim, first_all[1:-1], side_len)
    input_grad = input_side(first_all, weight_first, side_len)
    return (input_grad.transpose(1, 0, 2), reduce_parts(first_parts), reduce_parts(second_parts))


def solution(mesh):
    in_specs = (
        P("chan", "slab", None),
        P("chan", "slab", None),
        P("chan", "slab", None),
        P("chan", "slab", None),
        P(None, "chan", None),
        P(None, "chan", None),
    )
    out_specs = (P("chan", "slab", None), P(None, "chan", "slab"), P(None, "chan", "slab"))
    return jax.shard_map(
        per_device, mesh=mesh, in_specs=in_specs, out_specs=out_specs, check_vma=False
    )
```

profile of v0, /device:TPU:0, one launch (start us, length us, event | category | flops | bytes accessed | tf_op | source)
XLA Modules:
  0.0 779.0 jit_solution(15282233944061165967)
XLA Ops:
  10.4 4.9 collective-permute-start
  18.1 4.1 collective-permute-done.1
  24.3 4.3 collective-permute-start.4
  31.4 4.6 collective-permute-start.6
  38.5 4.4 collective-permute-done.7
  49.5 1.7 fusion.62
  55.0 4.4 all-gather.5.cloned.1.call-done
  59.4 5.4 copy.68
  64.8 6.4 fusion.119
  71.2 5.1 stack.25
  76.3 5.1 stack.24
  81.4 5.0 stack.26
  86.4 23.9 %fusion.27 = f32[1152,6,256]{0,2,1:T(8,128)S(1)} fusion(f32[3,1152,512,1]{2,1,0,3:T(8,128)} %bitcast.263, f32[1,6,512,256]{2,3,0,1:T(8,128)} %stack.26, f32[1,6,512,256]{2,3,0,1:T(8,128)} %stack.25, f32[1,6,512,256]{2,3,0,1:T(8,128)} %stack.24), kind=kOutput, calls=%fused_computation.25 | convolution fusion | flops 16312172544 | bytes 23592960 | tf_op jit(solution)/shard_map/dot_general | solution.py:54
  111.5 1.9 fusion.79
  113.4 3.4 collective-permute-start.2
  118.2 1.8 collective-permute-done.2
  120.0 4.1 collective-permute-done.3
  125.1 2.6 copy.70
  141.2 14.4 %fusion.102 = (f32[6,9,128,256]{2,3,0,1:T(8,128)}, f32[6,9,128,256]{2,3,0,1:T(8,128)}, f32[6,9,128,256]{2,3,0,1:T(8,128)}) fusion(f32[8,9,128,256]{2,3,0,1:T(8,128)} %get-tuple-element.105), kind=kLoop, calls=%fused_computation.190 | loop fusion | bytes 42467328 | tf_op jit(solution)/shard_map/slice | solution.py:77
  155.6 8.0 %copy.77 = f32[6,9,128,256]{3,2,1,0:T(8,128)} copy(f32[6,9,128,256]{2,3,0,1:T(8,128)} %get-tuple-element.23) | data formatting | bytes 14155776 | tf_op jit(solution)/shard_map/slice | solution.py:77
  163.6 8.0 %copy.76 = f32[6,9,128,256]{3,2,1,0:T(8,128)} copy(f32[6,9,128,256]{2,3,0,1:T(8,128)} %get-tuple-element.24) | data formatting | bytes 14155776 | tf_op jit(solution)/shard_map/slice | solution.py:77
  171.6 8.0 %copy.74 = f32[6,9,128,256]{3,2,1,0:T(8,128)} copy(f32[6,9,128,256]{2,3,0,1:T(8,128)} %get-tuple-element.25) | data formatting | bytes 14155776 | tf_op jit(solution)/shard_map/slice | solution.py:77
  179.7 3.1 copy.75
  182.8 9.1 %bitcast_multiply_fusion.3 = f32[9,128,512]{2,1,0:T(8,128)} fusion(f32[6,512,256,1]{2,1,3,0:T(8,128)S(1)} %bitcast.251, f32[6,9,128,256]{3,2,1,0:T(8,128)} %copy.77), kind=kOutput, calls=%fused_computation.38 | convolution fusion | flops 5436407808 | bytes 12582912 | tf_op jit(solution)/shard_map/dot_general | solution.py:76
  191.9 9.5 %bitcast_multiply_fusion.4 = f32[9,128,512]{2,1,0:T(8,128)} fusion(f32[6,512,256,1]{2,1,3,0:T(8,128)S(1)} %bitcast.252, f32[6,9,128,256]{3,2,1,0:T(8,128)} %copy.76), kind=kOutput, calls=%fused_computation.39 | convolution fusion | flops 5436407808 | bytes 12582912 | tf_op jit(solution)/shard_map/dot_general | solution.py:76
  201.4 7.1 bitcast_multiply_fusion.5
  208.6 5.4 copy.71
  213.9 5.4 reshape.545
  219.4 3.4 copy.95
  222.9 5.1 copy.96
  228.1 3.4 copy.97
  231.6 14.4 %fusion.101 = (f32[6,9,128,256]{2,3,0,1:T(8,128)}, f32[6,9,128,256]{2,3,0,1:T(8,128)}, f32[6,9,128,256]{2,3,0,1:T(8,128)}) fusion(f32[8,9,128,256]{2,3,0,1:T(8,128)} %get-tuple-element.104), kind=kLoop, calls=%fused_computation.189 | loop fusion | bytes 42467328 | tf_op jit(solution)/shard_map/slice | solution.py:77
  246.0 8.2 %copy.83 = f32[6,9,128,256]{3,2,1,0:T(8,128)} copy(f32[6,9,128,256]{2,3,0,1:T(8,128)} %get-tuple-element.20) | data formatting | bytes 14155776 | tf_op jit(solution)/shard_map/slice | solution.py:77
  254.1 9.0 %bitcast_multiply_fusion.2 = f32[9,128,512]{2,1,0:T(8,128)S(1)} fusion(f32[8,512,256]{1,2,0:T(8,128)} %reshape.545, f32[6,9,128,256]{3,2,1,0:T(8,128)} %copy.83), kind=kOutput, calls=%fused_computation.37 | convolution fusion | flops 5436407808 | bytes 12582912 | tf_op jit(solution)/shard_map/dot_general | solution.py:76
  263.1 3.5 copy.86
  266.7 8.1 %copy.87 = f32[6,9,128,256]{3,2,1,0:T(8,128)} copy(f32[6,9,128,256]{2,3,0,1:T(8,128)} %get-tuple-element.22) | data formatting | bytes 14155776 | tf_op jit(solution)/shard_map/slice | solution.py:77
  274.8 9.1 %bitcast_multiply_fusion.1 = f32[9,128,512]{2,1,0:T(8,128)S(1)} fusion(f32[8,512,256]{1,2,0:T(8,128)} %reshape.545, f32[6,9,128,256]{3,2,1,0:T(8,128)} %copy.87), kind=kOutput, calls=%fused_computation.36 | convolution fusion | flops 5436407808 | bytes 12582912 | tf_op jit(solution)/shard_map/dot_general | solution.py:76
  283.9 3.5 copy.90
  287.4 8.1 %copy.91 = f32[6,9,128,256]{3,2,1,0:T(8,128)} copy(f32[6,9,128,256]{2,3,0,1:T(8,128)} %get-tuple-element.21) | data formatting | bytes 14155776 | tf_op jit(solution)/shard_map/slice | solution.py:77
  295.5 9.0 %bitcast_multiply_fusion = f32[9,128,512]{2,1,0:T(8,128)S(1)} fusion(f32[8,512,256]{1,2,0:T(8,128)} %reshape.545, f32[6,9,128,256]{3,2,1,0:T(8,128)} %copy.91), kind=kOutput, calls=%fused_computation.35 | convolution fusion | flops 5436407808 | bytes 12582912 | tf_op jit(solution)/shard_map/dot_general | solution.py:76
  304.5 3.6 copy.94
  308.1 5.0 slice_bitcast_fusion.1
  313.1 23.3 %fusion.24 = f32[1152,6,256]{0,2,1:T(8,128)S(1)} fusion(f32[3,1152,512,1]{2,1,0,3:T(8,128)} %bitcast.264, f32[1,6,512,256]{2,3,0,1:T(8,128)S(1)} %get-tuple-element.59, f32[1,6,512,256]{2,3,0,1:T(8,128)S(1)} %get-tuple-element.60, f32[1,6,512,256]{2,3,0,1:T(8,128)S(1)} %get-tuple-element.58), kind=kOutput, calls=%fused_computation.24 | convolution fusion | flops 16312172544 | bytes 23592960 | tf_op jit(solution)/shard_map/dot_general | solution.py:54
  339.8 62.8 %reduce-scatter.15.cloned.1.call-done = f32[9,128,64]{1,0,2:T(8,128)} async-done(((f32[9,128,512]{1,0,2:T(8,128)}), f32[9,128,64]{1,0,2:T(8,128)}) %reduce-scatter.15.cloned.1.call-update) | async-done | bytes 294928 | tf_op jit(solution)/shard_map/reduce_scatter | solution.py:88
  402.7 91.4 %reduce-scatter.17.cloned.1.call-done = f32[9,128,64]{1,0,2:T(8,128)} async-done(((f32[9,128,512]{1,0,2:T(8,128)}), f32[9,128,64]{1,0,2:T(8,128)}) %reduce-scatter.17.cloned.1.call-update) | async-done | bytes 294928 | tf_op jit(solution)/shard_map/reduce_scatter | solution.py:88
  497.1 88.5 %reduce-scatter.7.cloned.1.call-done = f32[9,128,64]{1,0,2:T(8,128)} async-done(((f32[9,128,512]{1,0,2:T(8,128)}), f32[9,128,64]{1,0,2:T(8,128)}) %reduce-scatter.7.cloned.1.call-update) | async-done | bytes 294928 | tf_op jit(solution)/shard_map/reduce_scatter | solution.py:88
  585.6 91.6 %reduce-scatter.9.cloned.1.call-done = f32[9,128,64]{1,0,2:T(8,128)} async-done(((f32[9,128,512]{1,0,2:T(8,128)}), f32[9,128,64]{1,0,2:T(8,128)}) %reduce-scatter.9.cloned.1.call-update) | async-done | bytes 294928 | tf_op jit(solution)/shard_map/reduce_scatter | solution.py:88
  677.1 91.6 %reduce-scatter.11.cloned.1.call-done = f32[9,128,64]{1,0,2:T(8,128)} async-done(((f32[9,128,512]{1,0,2:T(8,128)}), f32[9,128,64]{1,0,2:T(8,128)}) %reduce-scatter.11.cloned.1.call-update) | async-done | bytes 294928 | tf_op jit(solution)/shard_map/reduce_scatter | solution.py:88
  (134 shorter events, 49.9 us)
Async XLA Ops:
  7.2 16.6 %copy-start.10 = (f32[128,6,256]{2,0,1:T(8,128)S(1)}, f32[128,6,256]{2,0,1:T(8,128)}, u32[]{:S(2)}) copy-start(f32[128,6,256]{2,0,1:T(8,128)} %param.7) | copy-start | bytes 2359300
  7.2 52.2 %all-gather.5.cloned.1.call-start = ((), (), s32[]{:S(2)}) async-start(), calls=%async_computation.12 | async-start | bytes 5242880 | tf_op jit(solution)/shard_map/all_gather | solution.py:45
  10.4 7.6 collective-permute-start
  15.3 6.9 collective-permute-start.1
  23.7 184.9 %all-gather.7.cloned.1.call-start = ((), (), s32[]{:S(2)}) async-start(), calls=%async_computation.13 | async-start | bytes 5242880 | tf_op jit(solution)/shard_map/all_gather | solution.py:45
  24.0 4.6 copy-start.4
  24.3 13.1 %collective-permute-start.4 = (f32[1,128,256]{1,2,0:T(8,128)S(1)}, f32[1,128,256]{1,2,0:T(8,128)S(1)}, u32[]{:S(2)}, u32[]{:S(2)}) collective-permute-start(f32[1,128,256]{1,2,0:T(8,128)S(1)} %get-tuple-element.98), channel_id=1, source_target_pairs={{0,4},{4,8},{8,12},{12,16},{16,20},{20,24},{24,28},{1,5},{5,9},{9,... | collective-permute-start | bytes 393224 | tf_op jit(solution)/shard_map/ppermute | solution.py:16
  28.6 8.8 %collective-permute-start.5 = (f32[1,128,256]{1,2,0:T(8,128)S(1)}, f32[1,128,256]{1,2,0:T(8,128)S(1)}, u32[]{:S(2)}, u32[]{:S(2)}) collective-permute-start(f32[1,128,256]{1,2,0:T(8,128)S(1)} %get-tuple-element.99), channel_id=1, source_target_pairs={{4,0},{8,4},{12,8},{16,12},{20,16},{24,20},{28,24},{5,1},{9,5},{13... | collective-permute-start | bytes 393224 | tf_op jit(solution)/shard_map/ppermute | solution.py:17
  31.4 6.0 copy-start.2
  31.4 7.1 collective-permute-start.6
  36.0 6.9 collective-permute-start.7
  110.3 1.1 copy-start.5
  113.4 6.5 collective-permute-start.2
  116.8 7.3 collective-permute-start.3
  127.7 212.1 %reduce-scatter.13.cloned.1.call-start = ((), (), s32[]{:S(2)}) async-start(), calls=%async_computation.9 | async-start | bytes 4718592 | tf_op jit(solution)/shard_map/reduce_scatter | solution.py:88
  127.8 0.8 copy-start.16
  127.8 0.9 copy-start.17
  130.4 3.1 copy-start.3
  130.7 5.5 copy-start.14
  130.7 5.5 copy-start.15
  132.4 5.4 copy-start.8
  132.4 5.4 copy-start.9
  132.4 5.4 copy-start.12
  132.4 5.4 copy-start.13
  133.5 6.1 copy-start.6
  133.5 6.1 copy-start.7
  133.5 6.1 copy-start.11
  182.8 18.6 %slice-start = ((s8[7077888]{0:T(1024)(128)(4,1)}), s8[4194304]{0:T(1024)(128)(4,1)S(1)}, s32[]{:S(2)}) async-start(s8[7077888]{0:T(1024)(128)(4,1)} %bitcast.255), calls=%async_computation.14 | async-start | bytes 8388608
  191.9 9.5 %slice-start.1 = ((s8[7077888]{0:T(1024)(128)(4,1)}), s8[2883584]{0:T(1024)(128)(4,1)S(1)}, s32[]{:S(2)}) async-start(s8[7077888]{0:T(1024)(128)(4,1)} %bitcast.255), calls=%async_computation.15 | async-start | bytes 5767168
  208.6 10.8 %copy-start.1 = (f32[9,128,512]{2,1,0:T(8,128)S(1)}, f32[9,128,512]{2,1,0:T(8,128)}, u32[]{:S(2)}) copy-start(f32[9,128,512]{2,1,0:T(8,128)} %bitcast_multiply_fusion.5) | copy-start | bytes 7077892
  222.8 5.2 copy-start
  222.9 179.8 %reduce-scatter.15.cloned.1.call-start = ((), (), s32[]{:S(2)}) async-start(), calls=%async_computation.10 | async-start | bytes 4718592 | tf_op jit(solution)/shard_map/reduce_scatter | solution.py:88
  228.0 266.1 %reduce-scatter.17.cloned.1.call-start = ((), (), s32[]{:S(2)}) async-start(), calls=%async_computation.11 | async-start | bytes 4718592 | tf_op jit(solution)/shard_map/reduce_scatter | solution.py:88
  231.5 354.0 %reduce-scatter.7.cloned.1.call-start = ((), (), s32[]{:S(2)}) async-start(), calls=%async_computation.6 | async-start | bytes 4718592 | tf_op jit(solution)/shard_map/reduce_scatter | solution.py:88
  266.6 410.5 %reduce-scatter.9.cloned.1.call-start = ((), (), s32[]{:S(2)}) async-start(), calls=%async_computation.7 | async-start | bytes 4718592 | tf_op jit(solution)/shard_map/reduce_scatter | solution.py:88
  287.3 481.4 %reduce-scatter.11.cloned.1.call-start = ((), (), s32[]{:S(2)}) async-start(), calls=%async_computation.8 | async-start | bytes 4718592 | tf_op jit(solution)/shard_map/reduce_scatter | solution.py:88
Sparse Core Ops, SparseCore 0:
  23.8 35.5 all-gather.4
  127.9 34.4 all-gather.6
  223.0 88.1 reduce-scatter.12
  314.7 87.9 reduce-scatter.14
  406.1 87.9 reduce-scatter.16
  497.6 87.9 reduce-scatter.6
  589.2 87.9 reduce-scatter.8
  680.8 87.9 reduce-scatter.10
where the time goes:
time: 784 us; the launch traced here: 779 us
  waiting for transfers between devices  447 us (57%)
  local copies, waits for them, and re-layouts  169 us (22%)
  matrix products  99.9 us (13%)
  other arithmetic  25 us (3%)
  starting transfers between devices  22.7 us (3%)
  between operations  15.2 us (2%)
    reduce_scatter x6, waiting for transfers between devices, reduce_parts(): lax.psum_scatter(part, 'slab', scatter_dimension=2, tiled=True)  426 us
    slice x8, local copies, waits for them, and re-layouts, weight_side(): moved[1 + a:1 + a + planes]  77.2 us
    dot_general x6, matrix products, weight_side(): lax.dot_general(moved[1 + a:1 + a + planes], centre, (((0, 2), (0, 2)), (...  52.7 us
    dot_general x2, matrix products, input_side(): lax.dot_general(rows, near, (((0, 2), (0, 2)), ((), ())), precision=lax.P...  47.2 us
    another operation x4, local copies, waits for them, and re-layouts, input_side(): near = jnp.stack([portion[1 - a:1 - a + planes] for a in STEPS], 0)  20.2 us
    ppermute x4, starting transfers between devices, with_rim(): before = lax.ppermute(value[-1:], 'slab', up)  17.2 us
  transfers between devices with their start and end apart: 16, of which 12 were waited for; matrix products, arithmetic and copies ran while one was open for 27% of the time, Pallas kernels for 0%

commit v1 on v0

v1 whole, which is shorter than its diff:
```python
import functools
import math

import jax
import jax.numpy as jnp
from jax import lax
from jax.experimental import pallas as pl
from jax.experimental.pallas import tpu as pltpu
from jax.sharding import PartitionSpec as P

F32 = jnp.float32
BF16 = jnp.bfloat16
MESH = pl.DeviceIdType.MESH
STEPS = (-1, 0, 1)
IN_PLANE = [(row_step, col_step) for row_step in STEPS for col_step in STEPS]


def silu_slope(values):
    sigma = jax.nn.sigmoid(values)
    return sigma * (1.0 + values * (1.0 - sigma))


def halves(value):
    high = value.astype(BF16)
    return high, (value - high.astype(F32)).astype(BF16)


def dot_nn(left, right):
    return lax.dot_general(left, right, (((1,), (0,)), ((), ())), preferred_element_type=F32)


def dot_nt(left, right):
    return lax.dot_general(left, right, (((1,), (1,)), ((), ())), preferred_element_type=F32)


def mega(
    dims,
    second_ref, hidden_ref, saved_ref, slope_ref, weight2_ref, weight1_ref,
    grad_ref, out1_ref, out2_ref,
    full, full_h, full_l, moved_h, moved_l, taps_h, taps_l, stage, raw, mixed,
    part2, part1, got2, got1,
    stage_sem, gather_send, gather_recv, rim_send, rim_recv, ring_send, ring_recv, free_sem,
):
    slabs, chans, total, planes, area, side = dims
    channels = total // chans
    block = total // slabs
    groups = 128 // block
    rows = len(IN_PLANE) * channels // groups
    cut = -(-rows // 16) * 8
    slices = ((0, cut), (cut, rows - cut))
    chips = chans // 2
    width = planes * area
    third = 3 * channels

    slab = lax.axis_index("slab")
    chan = lax.axis_index("chan")
    chip, core = chan // 2, chan % 2
    odd = slab % 2
    place = (1 - odd) * (slab // 2) + odd * (slabs - 1 - slab // 2)

    def slab_at(spot):
        upper = spot // (slabs // 2)
        return (1 - upper) * 2 * spot + upper * (2 * (slabs - 1 - spot) + 1)

    ring_next = slab_at((place + 1) % slabs)
    ring_prev = slab_at((place + slabs - 1) % slabs)
    partner = chip * 2 + 1 - core

    def far_chan(j):
        return ((chip + j) % chips) * 2 + core

    def near_chan(j):
        return ((chip + chips - j) % chips) * 2 + core

    has_left = slab > 0
    has_right = slab < slabs - 1
    rims = jnp.minimum(slab, 1) + jnp.minimum(slabs - 1 - slab, 1)

    def tell(semaphore):
        for j in range(1, chips):
            pl.semaphore_signal(semaphore, inc=1, device_id={"chan": far_chan(j)}, device_id_type=MESH)
        pl.semaphore_signal(semaphore, inc=1, device_id={"chan": partner}, device_id_type=MESH)

        @pl.when(has_left)
        def _():
            pl.semaphore_signal(semaphore, inc=1, device_id={"slab": slab - 1}, device_id_type=MESH)

        @pl.when(has_right)
        def _():
            pl.semaphore_signal(semaphore, inc=1, device_id={"slab": slab + 1}, device_id_type=MESH)

    barrier = pltpu.get_barrier_semaphore()
    tell(barrier)
    pl.semaphore_signal(barrier, inc=1, device_id={"slab": ring_next}, device_id_type=MESH)
    pl.semaphore_signal(barrier, inc=1, device_id={"slab": ring_prev}, device_id_type=MESH)
    pl.semaphore_wait(barrier, 2 + chips + rims)

    def chan_rows(index):
        return pl.ds(pl.multiple_of(index * channels, channels), channels)

    def lanes(slot, count=1):
        return pl.ds(pl.multiple_of(slot * area, area), count * area)

    mine = chan_rows(chan)

    def stage_copy(weight_ref, depth):
        return pltpu.make_async_copy(weight_ref.at[depth], stage, stage_sem.at[0])

    def rim_copy(layer, toward, source):
        slot = (0, planes + 1)[toward]
        target = (slab + 1, slab - 1)[toward]
        return pltpu.make_async_remote_copy(
            src_ref=source,
            dst_ref=full.at[mine, lanes(slot)],
            send_sem=rim_send.at[layer, toward],
            recv_sem=rim_recv.at[layer, toward],
            device_id={"slab": target},
            device_id_type=MESH,
        )

    def gather_copy(layer, slot, source, where, index, target):
        return pltpu.make_async_remote_copy(
            src_ref=source,
            dst_ref=full.at[where, lanes(slot)],
            send_sem=gather_send.at[layer, slot, index],
            recv_sem=gather_recv.at[layer, slot, index],
            device_id={"chan": target},
            device_id_type=MESH,
        )

    def gather_start(layer, slot, source):
        for j in range(1, chips):
            gather_copy(layer, slot, source, mine, j, far_chan(j)).start()
        gather_copy(layer, slot, source, mine, 0, partner).start()

    def gather_forward(layer, slot):
        for j in range(1, chips):
            where = chan_rows(near_chan(j))
            view = full.at[where, lanes(slot)]
            gather_copy(layer, slot, view, where, j, partner).wait_recv()
            gather_copy(layer, slot, view, where, chips + j, partner).start()

    def gather_finish(layer, slot):
        where = chan_rows(partner)
        gather_copy(layer, slot, full.at[where, lanes(slot)], where, 0, partner).wait_recv()
        for j in range(1, chips):
            where = chan_rows(((chip + chips - j) % chips) * 2 + 1 - core)
            gather_copy(layer, slot, full.at[where, lanes(slot)], where, chips + j, partner).wait_recv()

    def gather_sent(layer, slot):
        view = full.at[mine, lanes(slot)]
        for index in [*range(chips), *range(chips + 1, 2 * chips)]:
            gather_copy(layer, slot, view, mine, index, partner).wait_send()

    def rim_ends(layer, action):
        @pl.when(has_left)
        def _():
            action(0)

        @pl.when(has_right)
        def _():
            action(planes + 1)

    def rim_gather(layer):
        @pl.when(has_left)
        def _():
            rim_copy(layer, 0, full.at[mine, lanes(0)]).wait_recv()
            gather_start(layer, 0, full.at[mine, lanes(0)])

        @pl.when(has_right)
        def _():
            rim_copy(layer, 1, full.at[mine, lanes(planes + 1)]).wait_recv()
            gather_start(layer, planes + 1, full.at[mine, lanes(planes + 1)])

    def rim_sent(layer):
        @pl.when(has_right)
        def _():
            rim_copy(layer, 0, full.at[mine, lanes(0)]).wait_send()

        @pl.when(has_left)
        def _():
            rim_copy(layer, 1, full.at[mine, lanes(0)]).wait_send()

    def split_full(slot):
        @pl.loop(0, total // 32)
        def _(index):
            where = pl.ds(pl.multiple_of(index * 32, 32), 32)
            high, low = halves(full[where, lanes(slot)])
            full_h[where, lanes(slot)] = high
            full_l[where, lanes(slot)] = low

    def zero_slot(slot):
        @pl.loop(0, total // 32)
        def _(index):
            where = pl.ds(pl.multiple_of(index * 32, 32), 32)
            full_h[where, lanes(slot)] = jnp.zeros((32, area), BF16)
            full_l[where, lanes(slot)] = jnp.zeros((32, area), BF16)

    def split_all():
        @pl.loop(1, planes + 1)
        def _(slot):
            split_full(slot)

        @pl.when(has_left)
        def _():
            split_full(0)

        @pl.when(slab == 0)
        def _():
            zero_slot(0)

        @pl.when(has_right)
        def _():
            split_full(planes + 1)

        @pl.when(slab == slabs - 1)
        def _():
            zero_slot(planes + 1)

    cells = lax.broadcasted_iota(jnp.int32, (1, area), 1)
    row_ids, col_ids = cells // side, cells % side

    def mask_of(row_step, col_step):
        valid = (
            (row_ids + row_step >= 0)
            & (row_ids + row_step < side)
            & (col_ids + col_step >= 0)
            & (col_ids + col_step < side)
        )
        return jnp.where(valid, 1.0, 0.0).astype(F32)

    def shifted(value, row_step, col_step):
        if row_step == 0 and col_step == 0:
            return value
        shift = (-(row_step * side + col_step)) % area
        return pltpu.roll(value, shift, 1) * mask_of(row_step, col_step)

    def build_moved(source):
        @pl.loop(0, planes)
        def _(plane):
            @pl.loop(0, channels // 32)
            def _(index):
                start = pl.multiple_of(index * 32, 32)
                value = source[pl.ds(start, 32), lanes(plane)]
                for tap, (row_step, col_step) in enumerate(IN_PLANE):
                    high, low = halves(shifted(value, row_step, col_step))
                    where = pl.ds(pl.multiple_of(tap * channels + start, 32), 32)
                    moved_h[where, lanes(plane)] = high
                    moved_l[where, lanes(plane)] = low

    def split_taps(weight_ref):
        for depth in range(3):
            stage_copy(weight_ref, depth).wait()

            @pl.loop(0, 9 * channels // 48)
            def _(index):
                where = pl.ds(pl.multiple_of(index * 48, 48), 48)
                high, low = halves(stage[where, :])
                taps_h[depth, where, :] = high
                taps_l[depth, where, :] = low

            if depth < 2:
                stage_copy(weight_ref, depth + 1).start()

    parts = (part2, part1)
    gots = (got2, got1)
    outs = (out2_ref, out1_ref)

    def ring_copy(layer, flow, step, way, owner):
        span = pl.ds(*slices[way])
        return pltpu.make_async_remote_copy(
            src_ref=parts[layer].at[flow, owner, span],
            dst_ref=gots[layer].at[flow, step, span],
            send_sem=ring_send.at[layer, flow, step, way],
            recv_sem=ring_recv.at[layer, flow, step, way],
            device_id={"slab": (ring_next, ring_prev)[way]},
            device_id_type=MESH,
        )

    def ring_owner(step, way):
        if way == 0:
            return slab_at((place + 2 * slabs - 1 - step) % slabs)
        return slab_at((place + 1 + step) % slabs)

    def ring_first(layer, flow):
        for way in range(2):
            ring_copy(layer, flow, 0, way, ring_owner(0, way)).start()

    def ring_event(layer, flow, step):
        for way in range(2):
            owner = ring_owner(step, way)
            span = pl.ds(*slices[way])
            ring_copy(layer, flow, step - 1, way, owner).wait_recv()
            value = parts[layer][flow, owner, span] + gots[layer][flow, step - 1, span]

            @pl.when(step < slabs - 1)
            def _():
                parts[layer][flow, owner, span] = value
                ring_copy(layer, flow, step, way, owner).start()

            @pl.when(step == slabs - 1)
            def _():
                outs[layer][(flow + 1) % 3, span] = value

    def ring_tick(layer, tick):
        flow = (tick + 1) % 3
        ahead = tick - 2 - 4 * flow
        step = (ahead + 30) // 3 - 10

        @pl.when((ahead >= 3) & (step <= slabs - 1))
        def _():
            ring_event(layer, flow, step)

    last_tick = 10 + 3 * (slabs - 1)

    def pack(layer, flow):
        lane = lax.broadcasted_iota(jnp.int32, (1, 128), 1) // block

        @pl.loop(0, rows // 72)
        def _(index):
            start = index * 72
            for tile in range(total // 128):
                pieces = [
                    raw[pl.ds(pl.multiple_of(v * rows + start, 8), 72), pl.ds(tile * 128, 128)]
                    for v in range(groups)
                ]
                for u in range(groups):
                    value = None
                    for v in range(groups):
                        piece = pieces[v]
                        if u != v:
                            piece = pltpu.roll(piece, ((v - u) * block) % 128, 1)
                        value = piece if value is None else jnp.where(lane == v, piece, value)
                    parts[layer][flow, tile * groups + u, pl.ds(pl.multiple_of(start, 8), 72)] = value

    def weight_chunk(layer, tick):
        flow, third_index = tick // 3, tick % 3
        depth = (flow + 1) % 3
        where = pl.ds(pl.multiple_of(third_index * third, third), third)
        window = lanes(2 - depth, planes)
        value = dot_nt(moved_h[where, :], full_h[:, window])
        value += dot_nt(moved_h[where, :], full_l[:, window])
        value += dot_nt(moved_l[where, :], full_h[:, window])
        raw[where, :] = value

        @pl.when(third_index == 2)
        def _():
            pack(layer, flow)
            ring_first(layer, flow)

    def conv_plane(plane):
        value = jnp.zeros((9 * channels, area), F32)
        for depth in range(3):
            window = lanes(plane + 2 - depth)
            value += dot_nn(taps_h[depth], full_h[:, window])
            value += dot_nn(taps_h[depth], full_l[:, window])
            value += dot_nn(taps_l[depth], full_h[:, window])
        mixed[...] = value

    def conv_sum(finish):
        @pl.loop(0, channels // 32)
        def _(index):
            start = pl.multiple_of(index * 32, 32)
            value = jnp.zeros((32, area), F32)
            for tap, (row_step, col_step) in enumerate(IN_PLANE):
                where = pl.ds(pl.multiple_of(tap * channels + start, 32), 32)
                value += shifted(mixed[where, :], -row_step, -col_step)
            finish(start, value)

    stage_copy(weight2_ref, 0).start()

    @pl.when(has_right)
    def _():
        rim_copy(0, 0, second_ref.at[:, lanes(planes - 1)]).start()

    @pl.when(has_left)
    def _():
        rim_copy(0, 1, second_ref.at[:, lanes(0)]).start()

    for slot in range(1, planes + 1):
        gather_start(0, slot, second_ref.at[:, lanes(slot - 1)])
    for slot in range(1, planes + 1):
        full[mine, lanes(slot)] = second_ref[:, lanes(slot - 1)]
    split_taps(weight2_ref)
    stage_copy(weight1_ref, 0).start()
    rim_gather(0)
    build_moved(hidden_ref)
    for slot in range(1, planes + 1):
        gather_forward(0, slot)
    rim_ends(0, functools.partial(gather_forward, 0))
    for slot in range(1, planes + 1):
        gather_finish(0, slot)
    rim_ends(0, functools.partial(gather_finish, 0))
    split_all()
    for slot in range(1, planes + 1):
        gather_sent(0, slot)
    rim_ends(0, functools.partial(gather_sent, 0))
    rim_sent(0)
    tell(free_sem)

    @pl.loop(0, 9)
    def _(tick):
        weight_chunk(0, tick)
        ring_tick(0, tick)

    pl.semaphore_wait(free_sem, chips + rims)

    @pl.loop(0, planes)
    def _(index):
        plane = (index + planes - 1) % planes
        conv_plane(plane)

        def finish(start, value):
            where = pl.ds(start, 32)
            target = pl.ds(pl.multiple_of(chan * channels + start, 32), 32)
            full[target, lanes(plane + 1)] = value * slope_ref[where, lanes(plane)]

        conv_sum(finish)
        view = full.at[mine, lanes(plane + 1)]

        @pl.when((plane == planes - 1) & has_right)
        def _():
            rim_copy(1, 0, view).start()

        @pl.when((plane == 0) & has_left)
        def _():
            rim_copy(1, 1, view).start()

        gather_start(1, plane + 1, view)

        @pl.when(index > 0)
        def _():
            gather_forward(1, (index + planes - 2) % planes + 1)

        @pl.when(index == 2)
        def _():
            rim_gather(1)

        @pl.when(index == planes - 1)
        def _():
            rim_ends(1, functools.partial(gather_forward, 1))

        ring_tick(0, index + 9)

    base = 9 + planes + 3
    build_moved(saved_ref)
    ring_tick(0, base - 3)
    gather_forward(1, planes - 1)
    split_taps(weight1_ref)
    ring_tick(0, base - 2)
    for slot in range(1, planes + 1):
        gather_finish(1, slot)
    rim_ends(1, functools.partial(gather_finish, 1))
    split_all()
    ring_tick(0, base - 1)

    @pl.loop(0, 9)
    def _(tick):
        weight_chunk(1, tick)
        ring_tick(0, base + tick)
        ring_tick(1, tick)

    @pl.loop(0, planes)
    def _(plane):
        conv_plane(plane)

        def finish(start, value):
            grad_ref[pl.ds(start, 32), lanes(plane)] = value

        conv_sum(finish)
        ring_tick(0, base + 9 + plane)
        ring_tick(1, 9 + plane)

    @pl.loop(9 + planes, last_tick + 1)
    def _(tick):
        ring_tick(0, base + tick)
        ring_tick(1, tick)

    for slot in range(1, planes + 1):
        gather_sent(1, slot)
    rim_ends(1, functools.partial(gather_sent, 1))
    rim_sent(1)
    for layer in range(2):
        for way in range(2):
            @pl.loop(0, 3)
            def _(flow):
                @pl.loop(0, slabs - 1)
                def _(step):
                    ring_copy(layer, flow, step, way, 0).wait_send()


def per_device(saved_input, pre_first, pre_second, out_grad, weight_first, weight_second):
    channels, planes, area = saved_input.shape
    total = weight_first.shape[2]
    slabs, chans = lax.axis_size("slab"), lax.axis_size("chan")
    side = math.isqrt(area)
    block = total // slabs
    groups = 128 // block
    rows = 9 * channels // groups
    width = planes * area
    flat = (channels, width)
    dims = (slabs, chans, total, planes, area, side)

    second_grad = (out_grad * silu_slope(pre_second)).reshape(flat)
    hidden = jax.nn.silu(pre_first).reshape(flat)
    slope = silu_slope(pre_first).reshape(flat)
    saved = saved_input.reshape(flat)
    wide = (planes + 2) * area
    chips = chans // 2
    vmem = pl.BlockSpec(memory_space=pltpu.VMEM)
    hbm = pl.BlockSpec(memory_space=pl.ANY)
    out_part = jax.ShapeDtypeStruct((3, rows, 128), F32)
    input_grad, first, second = pl.pallas_call(
        functools.partial(mega, dims),
        out_shape=(jax.ShapeDtypeStruct(flat, F32), out_part, out_part),
        in_specs=[vmem] * 4 + [hbm] * 2,
        out_specs=(vmem, vmem, vmem),
        scratch_shapes=[
            pltpu.VMEM((total, wide), F32),
            pltpu.VMEM((total, wide), BF16),
            pltpu.VMEM((total, wide), BF16),
            pltpu.VMEM((9 * channels, width), BF16),
            pltpu.VMEM((9 * channels, width), BF16),
            pltpu.VMEM((3, 9 * channels, total), BF16),
            pltpu.VMEM((3, 9 * channels, total), BF16),
            pltpu.VMEM((9 * channels, total), F32),
            pltpu.VMEM((9 * channels, total), F32),
            pltpu.VMEM((9 * channels, area), F32),
            pltpu.VMEM((3, slabs, rows, 128), F32),
            pltpu.VMEM((3, slabs, rows, 128), F32),
            pltpu.VMEM((3, slabs - 1, rows, 128), F32),
            pltpu.VMEM((3, slabs - 1, rows, 128), F32),
            pltpu.SemaphoreType.DMA((1,)),
            pltpu.SemaphoreType.DMA((2, planes + 2, 2 * chips)),
            pltpu.SemaphoreType.DMA((2, planes + 2, 2 * chips)),
            pltpu.SemaphoreType.DMA((2, 2)),
            pltpu.SemaphoreType.DMA((2, 2)),
            pltpu.SemaphoreType.DMA((2, 3, slabs - 1, 2)),
            pltpu.SemaphoreType.DMA((2, 3, slabs - 1, 2)),
            pltpu.SemaphoreType.REGULAR,
        ],
        compiler_params=pltpu.CompilerParams(
            collective_id=0, has_side_effects=True, vmem_limit_bytes=67043328
        ),
        name="backward",
    )(
        second_grad, hidden, saved, slope,
        weight_second.reshape(3, 9 * channels, total),
        weight_first.reshape(3, 9 * channels, total),
    )
    scale = math.sqrt(planes * slabs * area)

    def unpack(packed):
        value = packed.reshape(3, rows, groups, block).transpose(0, 2, 1, 3)
        return value.reshape(27, channels, block) / scale

    return input_grad.reshape(channels, planes, area), unpack(first), unpack(second)


def solution(mesh):
    in_specs = (
        P("chan", "slab", None),
        P("chan", "slab", None),
        P("chan", "slab", None),
        P("chan", "slab", None),
        P(None, "chan", None),
        P(None, "chan", None),
    )
    out_specs = (P("chan", "slab", None), P(None, "chan", "slab"), P(None, "chan", "slab"))
    return jax.shard_map(
        per_device, mesh=mesh, in_specs=in_specs, out_specs=out_specs, check_vma=False
    )
```

time: 784 us -> 220 us (0.28)
  waiting for transfers between devices: 447 us -> 0 us
  Pallas kernels: 0 us -> 198 us
  local copies, waits for them, and re-layouts: 169 us -> 19.2 us
  matrix products: 99.9 us -> 0 us
  other arithmetic: 25 us -> 2.17 us
  starting transfers between devices: 22.7 us -> 0 us
  between operations: 15.2 us -> 0.72 us
    reduce_scatter x6 -> x0, waiting for transfers between devices: 426 us -> none  [reduce_parts(): lax.psum_scatter(part, 'slab', scatter_dimension=2, tiled=True)]
    pallas_call x0 -> x1, Pallas kernels: none -> 198 us  [per_device(): pl.pallas_call(functools.partial(mega, dims), out_shape=(jax.ShapeDtypeSt...]
    dot_general x8 -> x0, matrix products: 99.9 us -> none  [the longest x6 52.7 us: weight_side(): lax.dot_general(moved[1 + a:1 + a + planes], centre, (((0, 2), (0, 2)), (...]
    slice x30 -> x0, local copies, waits for them, and re-layouts: 87.8 us -> none  [the longest x8 77.2 us: weight_side(): moved[1 + a:1 + a + planes]]
    ppermute x8 -> x0, starting transfers between devices: 22.3 us -> none  [the longest x4 17.2 us: with_rim(): before = lax.ppermute(value[-1:], 'slab', up)]
    another operation x4 -> x0, local copies, waits for them, and re-layouts: 20.2 us -> none  [input_side(): near = jnp.stack([portion[1 - a:1 - a + planes] for a in STEPS], 0)]
    ppermute x8 -> x0, waiting for transfers between devices: 16.9 us -> none  [the longest x4 12.7 us: with_rim(): after = lax.ppermute(value[:1], 'slab', down)]
    unnamed x10 -> x0, other arithmetic: 13.8 us -> none
  transfers between devices with their start and end apart: 16 -> 0, of which waited for: 12 -> 0; matrix products, arithmetic and copies ran while one was open for 27% -> 0% of each run, Pallas kernels for 0% -> 0%
where the time goes in v1:
time: 220 us
  Pallas kernels  198 us (90%)
  local copies, waits for them, and re-layouts  19.2 us (9%)
    pallas_call x1, Pallas kernels, per_device(): pl.pallas_call(functools.partial(mega, dims), out_shape=(jax.ShapeDtypeSt...  198 us
    unnamed x7, local copies, waits for them, and re-layouts  9.59 us

profile of v1, /device:TPU:0, one launch (start us, length us, event | category | flops | bytes accessed | tf_op | source)
XLA Modules:
  0.0 219.8 jit_solution(7817643052198937047)
XLA Ops:
  0.6 1.4 copy.19
  2.0 1.2 copy.23.saved_ref
  3.2 1.4 copy.18
  4.6 1.4 copy.14
  6.0 1.4 copy.16
  7.4 0.3 multiply_multiply_fusion
  7.7 1.1 copy.21.second_ref
  8.8 0.3 add_multiply_fusion
  9.1 1.1 copy.24.slope_ref
  10.3 1.1 copy.22.hidden_ref
  11.4 197.7 %backward.1 = (f32[128,1536]{1,0:T(8,128)}, f32[3,576,128]{2,1,0:T(8,128)}, f32[3,576,128]{2,1,0:T(8,128)}) custom-call(f32[128,1536]{1,0:T(8,128)} %copy.21.second_ref, f32[128,1536]{1,0:T(8,128)} %copy.22.hidden_ref, f32[128,1536]{1,0:T(8,128)} %copy.23.saved_ref, f32[128,1536]{1,0:T(8,128)} %copy.24.slope_ref, f32[3,1152,512]{2,1,0:T(8,128)} %bitcast.17, ...), custom_call_target="tpu_custom_call" | custom-call | tf_op jit(solution)/shard_map/backward/pallas_call | solution.py:513
  209.1 1.4 copy.25
  210.5 1.2 copy.30
  211.6 1.6 broadcast_multiply_fusion
  213.2 0.3 copy.28
  213.6 0.8 copy.29
  214.3 0.7 div.35
  215.1 1.4 copy.32
  216.5 0.3 copy.26
  216.8 0.8 copy.27
  217.6 0.7 div.31
  218.4 1.4 copy.31

commit v2 on v0

v2 whole, which is shorter than its diff:
```python
import functools
import math

import jax
import jax.numpy as jnp
from jax import lax
from jax.experimental import pallas as pl
from jax.experimental.pallas import tpu as pltpu
from jax.sharding import PartitionSpec as P

F32 = jnp.float32
BF16 = jnp.bfloat16
MESH = pl.DeviceIdType.MESH
STEPS = (-1, 0, 1)
EVENTS = (
    ((1, 0, 2), (0, 1, 5)),
    ((1, 0, 3),),
    ((1, 1, 0),),
    ((1, 0, 4),),
    ((1, 1, 1),),
    ((1, 0, 5), (1, 1, 2)),
    ((1, 1, 3), (1, 1, 4), (1, 1, 5)),
)
IN_PLANE = [(row_step, col_step) for row_step in STEPS for col_step in STEPS]


def silu_slope(values):
    sigma = jax.nn.sigmoid(values)
    return sigma * (1.0 + values * (1.0 - sigma))


def halves(value):
    high = value.astype(BF16)
    return high, (value - high.astype(F32)).astype(BF16)


def dot_nn(left, right):
    return lax.dot_general(left, right, (((1,), (0,)), ((), ())), preferred_element_type=F32)


def dot_nt(left, right):
    return lax.dot_general(left, right, (((1,), (1,)), ((), ())), preferred_element_type=F32)


def mega(
    dims,
    saved_hbm, first_hbm, second_hbm, out_hbm, weight1_ref, weight2_ref,
    grad_ref, out1_ref, out2_ref,
    raw_second, raw_first, raw_out, sent, hidden, other2, other1,
    full, far, full_h, full_l, near_h, near_l, moved_h, moved_l, taps_h, taps_l,
    stage, raw, mixed, part2, part1, gotw2, gotw1, gotd2, gotd1, final,
    load_sem, stage_sem, gather_send, gather_recv, rim_send, rim_recv, pair_send, pair_recv,
    other_send, other_recv, wide_send, wide_recv, deep_send, deep_recv, store_sem, free_sem, slot_sem,
):
    slabs, chans, total, planes, area, side = dims
    channels = total // chans
    block = total // slabs
    groups = 128 // block
    rows = len(IN_PLANE) * channels // groups // 2
    chips = chans // 2
    members = slabs // 4
    owned = 2 * block
    half = total // 2
    width = planes * area
    wide = (planes + 2) * area
    steps = 9 * channels
    lump = steps // 2

    slab = lax.axis_index("slab")
    chan = lax.axis_index("chan")
    chip, core = chan // 2, chan % 2
    deep, across = slab // 2, slab % 2
    parity, member = deep % 2, deep // 2
    pair = slab + 2 - 4 * parity
    beside = slab + 1 - 2 * across
    partner = chip * 2 + 1 - core

    def kind_of(index):
        return (index * slabs // (2 * chans)) % 2

    takes = kind_of(chan) == parity
    gives = kind_of(chan) != parity

    def far_chan(j):
        return ((chip + j) % chips) * 2 + core

    def near_chan(j):
        return ((chip + chips - j) % chips) * 2 + core

    def crossed_chan(j):
        return ((chip + chips - j) % chips) * 2 + 1 - core

    def deep_slab(j):
        return 2 * (2 * ((member + j) % members) + parity) + across

    has_left = slab > 0
    has_right = slab < slabs - 1
    rims = jnp.minimum(slab, 1) + jnp.minimum(slabs - 1 - slab, 1)

    def signal(semaphore, **target):
        pl.semaphore_signal(semaphore, inc=1, device_id=target, device_id_type=MESH)

    def tell(semaphore):
        for j in range(1, chips):
            signal(semaphore, chan=far_chan(j))
        signal(semaphore, chan=partner)
        signal(semaphore, slab=pair)

        @pl.when(has_left)
        def _():
            signal(semaphore, slab=slab - 1)

        @pl.when(has_right)
        def _():
            signal(semaphore, slab=slab + 1)

    def load_copy(index):
        source = (second_hbm, out_hbm, first_hbm, saved_hbm)[index]
        target = (raw_second, raw_out, raw_first, raw_second)[index]
        return pltpu.make_async_copy(source, target, load_sem.at[index])

    def stage_copy(weight_ref, piece):
        source = weight_ref.at[piece // 2, pl.ds(piece % 2 * lump, lump)]
        return pltpu.make_async_copy(source, stage.at[piece % 2], stage_sem.at[piece % 2])

    for index in range(3):
        load_copy(index).start()
    stage_copy(weight2_ref, 0).start()
    stage_copy(weight2_ref, 1).start()

    barrier = pltpu.get_barrier_semaphore()
    tell(barrier)
    signal(barrier, slab=beside)
    for j in range(1, members):
        signal(barrier, slab=deep_slab(j))
    pl.semaphore_wait(barrier, 1 + members + chips + rims)

    def chan_rows(index):
        return pl.ds(pl.multiple_of(index * channels, channels), channels)

    def far_rows(index):
        start = index * channels
        group = start // (2 * owned)
        inside = start - (2 * group + kind_of(index)) * owned
        return pl.ds(pl.multiple_of(group * owned + inside, channels), channels)

    def lanes(slot, count=1):
        return pl.ds(pl.multiple_of(slot * area, area), count * area)

    mine = chan_rows(chan)

    def exists(kind, slot):
        base = (slab, pair)[kind]
        return (slot + base > 0) & (slot - (planes + 1) + base < slabs - 1)

    def rim_copy(layer, toward, source):
        return pltpu.make_async_remote_copy(
            src_ref=source,
            dst_ref=full.at[mine, lanes((0, planes + 1)[toward])],
            send_sem=rim_send.at[layer, toward],
            recv_sem=rim_recv.at[layer, toward],
            device_id={"slab": (slab + 1, slab - 1)[toward]},
            device_id_type=MESH,
        )

    def rim_start(layer):
        @pl.when(has_right)
        def _():
            rim_copy(layer, 0, sent.at[:, lanes(planes - 1)]).start()

        @pl.when(has_left)
        def _():
            rim_copy(layer, 1, sent.at[:, lanes(0)]).start()

    def rim_sent(layer):
        @pl.when(has_right)
        def _():
            rim_copy(layer, 0, sent.at[:, lanes(0)]).wait_send()

        @pl.when(has_left)
        def _():
            rim_copy(layer, 1, sent.at[:, lanes(0)]).wait_send()

    def pair_copy(layer, slot, source):
        return pltpu.make_async_remote_copy(
            src_ref=source,
            dst_ref=far.at[far_rows(chan), lanes(slot)],
            send_sem=pair_send.at[layer, slot],
            recv_sem=pair_recv.at[layer, slot],
            device_id={"slab": pair},
            device_id_type=MESH,
        )

    def other_copy(layer):
        return pltpu.make_async_remote_copy(
            src_ref=hidden,
            dst_ref=(other2, other1)[layer],
            send_sem=other_send.at[layer],
            recv_sem=other_recv.at[layer],
            device_id={"slab": pair},
            device_id_type=MESH,
        )

    def gather_copy(layer, kind, slot, source, owner, index, target):
        where = (chan_rows, far_rows)[kind](owner)
        return pltpu.make_async_remote_copy(
            src_ref=source,
            dst_ref=(full, far)[kind].at[where, lanes(slot)],
            send_sem=gather_send.at[layer, kind, slot, index],
            recv_sem=gather_recv.at[layer, kind, slot, index],
            device_id={"chan": target},
            device_id_type=MESH,
        )

    def held(kind, owner, slot):
        if kind == 0:
            return full.at[chan_rows(owner), lanes(slot)]
        return far.at[far_rows(owner), lanes(slot)]

    def guard(kind, owner):
        if kind == 0:
            return lambda action: action()
        return pl.when(kind_of(owner) == parity)

    def gather_start(layer, kind, slot, source):
        for j in range(1, chips):
            gather_copy(layer, kind, slot, source, chan, j, far_chan(j)).start()
        gather_copy(layer, kind, slot, source, chan, 0, partner).start()

    def gather_forward(layer, kind, slot):
        for j in range(1, chips):
            owner = near_chan(j)

            @guard(kind, owner)
            def _():
                view = held(kind, owner, slot)
                gather_copy(layer, kind, slot, view, owner, j, partner).wait_recv()
                gather_copy(layer, kind, slot, view, owner, chips + j, partner).start()

    def gather_finish(layer, kind, slot):
        @guard(kind, partner)
        def _():
            gather_copy(layer, kind, slot, held(kind, partner, slot), partner, 0, partner).wait_recv()

        for j in range(1, chips):
            owner = crossed_chan(j)

            @guard(kind, owner)
            def _():
                view = held(kind, owner, slot)
                gather_copy(layer, kind, slot, view, owner, chips + j, partner).wait_recv()

    def gather_sent(layer, kind, slot):
        @guard(kind, chan)
        def _():
            for index in range(chips):
                view = held(kind, chan, slot)
                gather_copy(layer, kind, slot, view, chan, index, partner).wait_send()

        for j in range(1, chips):
            owner = near_chan(j)

            @guard(kind, owner)
            def _():
                view = held(kind, owner, slot)
                gather_copy(layer, kind, slot, view, owner, chips + j, partner).wait_send()

    def slots_loop(action):
        @pl.loop(0, planes + 2)
        def _(index):
            action((index + 1) % (planes + 2))

    def when_exists(action, layer, kind):
        def run(slot):
            @pl.when(exists(kind, slot))
            def _():
                action(layer, kind, slot)

        return run

    def send_slot(layer, slot):
        gather_start(layer, 0, slot, sent.at[:, lanes(slot - 1)])

    def send_pair(layer, slot):
        @pl.when(gives)
        def _():
            pair_copy(layer, slot, sent.at[:, lanes(slot - 1)]).start()

    def rim_spread(layer):
        for toward in range(2):
            slot = (0, planes + 1)[toward]

            @pl.when((has_left, has_right)[toward])
            def _():
                view = full.at[mine, lanes(slot)]
                rim_copy(layer, toward, view).wait_recv()
                gather_start(layer, 0, slot, view)

                @pl.when(gives)
                def _():
                    pair_copy(layer, slot, view).start()

    def far_start(layer, kind, slot):
        @pl.when(takes)
        def _():
            view = held(1, chan, slot)
            pair_copy(layer, slot, view).wait_recv()
            gather_start(layer, 1, slot, view)

    def pair_sent(layer, slot):
        @pl.when(gives)
        def _():
            pair_copy(layer, slot, sent.at[:, lanes(0)]).wait_send()

    def slot_sent(layer, kind, slot):
        gather_sent(layer, 0, slot)
        pair_sent(layer, slot)

    def split_rows(source, start, high_ref, low_ref, target, slot):
        high, low = halves(source[pl.ds(start, 32), lanes(slot)])
        high_ref[pl.ds(target, 32), lanes(slot)] = high
        low_ref[pl.ds(target, 32), lanes(slot)] = low

    def split_full(slot):
        @pl.when(exists(0, slot))
        def _():
            @pl.loop(0, total // 32)
            def _(index):
                start = pl.multiple_of(index * 32, 32)
                split_rows(full, start, full_h, full_l, start, slot)

        @pl.when(jnp.logical_not(exists(0, slot)))
        def _():
            @pl.loop(0, total // 32)
            def _(index):
                where = pl.ds(pl.multiple_of(index * 32, 32), 32)
                full_h[where, lanes(slot)] = jnp.zeros((32, area), BF16)
                full_l[where, lanes(slot)] = jnp.zeros((32, area), BF16)

    def copy_near():
        @pl.loop(0, half // 32)
        def _(index):
            start = pl.multiple_of(index * 32, 32)
            group = start // owned
            where = pl.ds(pl.multiple_of(start + (group + parity) * owned, 32), 32)
            near_h[0, pl.ds(start, 32), :] = full_h[where, :]
            near_l[0, pl.ds(start, 32), :] = full_l[where, :]

    def split_far(slot):
        @pl.when(exists(1, slot))
        def _():
            @pl.loop(0, half // 32)
            def _(index):
                start = pl.multiple_of(index * 32, 32)
                split_rows(far, start, near_h.at[1], near_l.at[1], start, slot)

        @pl.when(jnp.logical_not(exists(1, slot)))
        def _():
            @pl.loop(0, half // 32)
            def _(index):
                where = pl.ds(pl.multiple_of(index * 32, 32), 32)
                near_h[1, where, lanes(slot)] = jnp.zeros((32, area), BF16)
                near_l[1, where, lanes(slot)] = jnp.zeros((32, area), BF16)

    cells = lax.broadcasted_iota(jnp.int32, (1, area), 1)
    row_ids, col_ids = cells // side, cells % side

    def mask_of(row_step, col_step):
        valid = (
            (row_ids + row_step >= 0)
            & (row_ids + row_step < side)
            & (col_ids + col_step >= 0)
            & (col_ids + col_step < side)
        )
        return jnp.where(valid, 1.0, 0.0).astype(F32)

    def shifted(value, row_step, col_step):
        if row_step == 0 and col_step == 0:
            return value
        shift = (-(row_step * side + col_step)) % area
        return pltpu.roll(value, shift, 1) * mask_of(row_step, col_step)

    def build_moved(piece, source):
        @pl.loop(0, planes)
        def _(plane):
            @pl.loop(0, channels // 32)
            def _(index):
                start = pl.multiple_of(index * 32, 32)
                value = source[pl.ds(start, 32), lanes(plane)]
                for tap, (row_step, col_step) in enumerate(IN_PLANE):
                    high, low = halves(shifted(value, row_step, col_step))
                    where = pl.ds(pl.multiple_of(tap * channels + start, 32), 32)
                    moved_h[piece, where, lanes(plane)] = high
                    moved_l[piece, where, lanes(plane)] = low

    def split_taps(weight_ref):
        for piece in range(6):
            stage_copy(weight_ref, piece).wait()

            @pl.loop(0, lump // 48)
            def _(index):
                start = pl.multiple_of(index * 48, 48)
                high, low = halves(stage[piece % 2, pl.ds(start, 48), :])
                where = pl.ds(pl.multiple_of(piece % 2 * lump + start, 48), 48)
                taps_h[piece // 2, where, :] = high
                taps_l[piece // 2, where, :] = low

            if piece < 4:
                stage_copy(weight_ref, piece + 2).start()

    parts, gotw, gotd = (part2, part1), (gotw2, gotw1), (gotd2, gotd1)
    outs = (out2_ref, out1_ref)

    def wide_copy(layer, flow):
        return pltpu.make_async_remote_copy(
            src_ref=parts[layer].at[flow, 1 - across],
            dst_ref=gotw[layer].at[flow],
            send_sem=wide_send.at[layer, flow],
            recv_sem=wide_recv.at[layer, flow],
            device_id={"slab": beside},
            device_id_type=MESH,
        )

    def deep_copy(layer, flow, j):
        return pltpu.make_async_remote_copy(
            src_ref=parts[layer].at[flow, across, (member + j) % members],
            dst_ref=gotd[layer].at[flow, j - 1],
            send_sem=deep_send.at[layer, flow, j - 1],
            recv_sem=deep_recv.at[layer, flow, j - 1],
            device_id={"slab": deep_slab(j)},
            device_id_type=MESH,
        )

    def store_copy(layer, flow):
        depth, where = (flow // 2 + 1) % 3, pl.ds(flow % 2 * lump, lump)
        return pltpu.make_async_copy(
            final.at[flow], outs[layer].at[depth, where], store_sem.at[layer, flow]
        )

    def rows_loop(action):
        if rows % 72:
            action(0, rows)
        else:

            @pl.loop(0, rows // 72)
            def _(part):
                action(pl.multiple_of(part * 72, 8), 72)

    def wide_event(layer, flow):
        wide_copy(layer, flow).wait_recv()
        for j in [*range(1, members), 0]:
            index = (member + j) % members

            def add(start, count):
                where = pl.ds(start, count)
                parts[layer][flow, across, index, where] = (
                    parts[layer][flow, across, index, where] + gotw[layer][flow, index, where]
                )

            rows_loop(add)
            if j:
                deep_copy(layer, flow, j).start()

    def deep_event(layer, flow):
        for j in range(1, members):
            deep_copy(layer, flow, j).wait_recv()
        if layer:
            store_copy(0, flow).wait()

        def add(start, count):
            where = pl.ds(start, count)
            value = parts[layer][flow, across, member, where]
            for j in range(1, members):
                value += gotd[layer][flow, j - 1, where]
            for v in range(groups):
                piece = pltpu.roll(value, (128 - v * block) % 128, 1) if v else value
                final[flow, pl.ds(v * rows + start, count), :] = piece[:, :block]

        rows_loop(add)
        store_copy(layer, flow).start()

    def pack(layer, flow):
        lane = lax.broadcasted_iota(jnp.int32, (1, 128), 1) // block

        def move(start, count):
            for tile in range(half // 128):
                pieces = [
                    raw[pl.ds(v * rows + start, count), pl.ds(tile * 128, 128)]
                    for v in range(groups)
                ]
                for u in range(groups):
                    value = None
                    for v in range(groups):
                        piece = pieces[v]
                        if u != v:
                            piece = pltpu.roll(piece, ((v - u) * block) % 128, 1)
                        value = piece if value is None else jnp.where(lane == v, piece, value)
                    owner = tile * groups + u
                    parts[layer][flow, owner % 2, owner // 2, pl.ds(start, count)] = value

        rows_loop(move)

    def weight_part(layer, flow):
        depth = (flow // 2 + 1) % 3
        window = lanes(2 - depth, planes)
        where = pl.ds(pl.multiple_of(flow % 2 * lump, lump), lump)
        value = jnp.zeros((lump, half), F32)
        for piece in range(2):
            value += dot_nt(moved_h[piece, where, :], near_h[piece, :, window])
            value += dot_nt(moved_h[piece, where, :], near_l[piece, :, window])
            value += dot_nt(moved_l[piece, where, :], near_h[piece, :, window])
        raw[...] = value
        pack(layer, flow)
        wide_copy(layer, flow).start()

    def conv_plane(plane):
        value = jnp.zeros((steps, area), F32)
        for depth in range(3):
            window = lanes(plane + 2 - depth)
            value += dot_nn(taps_h[depth], full_h[:, window])
            value += dot_nn(taps_h[depth], full_l[:, window])
            value += dot_nn(taps_l[depth], full_h[:, window])
        mixed[...] = value

    def conv_sum(finish):
        @pl.loop(0, channels // 32)
        def _(index):
            start = pl.multiple_of(index * 32, 32)
            value = jnp.zeros((32, area), F32)
            for tap, (row_step, col_step) in enumerate(IN_PLANE):
                where = pl.ds(pl.multiple_of(tap * channels + start, 32), 32)
                value += shifted(mixed[where, :], -row_step, -col_step)
            finish(start, value)

    def each_plane(action):
        @pl.loop(0, planes)
        def _(plane):
            @pl.loop(0, channels // 32)
            def _(index):
                action(plane, pl.ds(pl.multiple_of(index * 32, 32), 32))

    load_copy(0).wait()
    load_copy(1).wait()

    def make_sent(plane, where):
        sent[where, lanes(plane)] = raw_out[plane, where, :] * silu_slope(raw_second[plane, where, :])

    each_plane(make_sent)
    rim_start(0)
    for slot in range(1, 4):
        send_slot(0, slot)
    for slot in range(1, planes + 1):
        send_pair(0, slot)
    load_copy(3).start()
    load_copy(2).wait()

    def make_hidden(plane, where):
        value = raw_first[plane, where, :]
        hidden[where, lanes(plane)] = value * jax.nn.sigmoid(value)

    each_plane(make_hidden)

    def keep_sent(plane, where):
        target = pl.ds(pl.multiple_of(chan * channels + where.start, 32), 32)
        full[target, lanes(plane + 1)] = sent[where, lanes(plane)]

    each_plane(keep_sent)
    split_taps(weight2_ref)
    stage_copy(weight1_ref, 0).start()
    stage_copy(weight1_ref, 1).start()
    for slot in range(4, planes + 1):
        send_slot(0, slot)
    rim_spread(0)
    build_moved(0, hidden)
    other_copy(0).start()
    for slot in (1, 2):
        gather_forward(0, 0, slot)
    gather_forward(0, 0, 3)
    for slot in (1, 2):
        gather_finish(0, 0, slot)
        split_full(slot)

    def when_far(action, layer):
        return when_exists(action, layer, 1)

    def make_saved(plane, where):
        hidden[where, lanes(plane)] = raw_second[plane, where, :]

    @pl.loop(0, planes)
    def _(index):
        plane = (index + 1) % planes
        slot = (index + 3) % (planes + 2)

        @pl.when(exists(0, slot))
        def _():
            gather_finish(0, 0, slot)

        split_full(slot)
        slot_sent(0, 0, plane + 1)
        for j in range(1, chips):
            signal(slot_sem.at[plane], chan=far_chan(j))
        signal(slot_sem.at[plane], chan=partner)
        conv_plane(plane)
        following = (index + 4) % (planes + 2)

        @pl.when((index < planes - 1) & exists(0, following))
        def _():
            gather_forward(0, 0, following)

        @pl.when(index == 0)
        def _():
            for late in range(1, planes + 1):
                far_start(0, 1, late)
            for late in (planes + 1, 0):
                when_far(far_start, 0)(late)

        @pl.when(index == planes - 2)
        def _():
            load_copy(3).wait()
            other_copy(0).wait_send()
            each_plane(make_saved)
            other_copy(1).start()

        @pl.when((plane == 0) & has_left)
        def _():
            rim_copy(0, 1, sent.at[:, lanes(0)]).wait_send()

        @pl.when((plane == planes - 1) & has_right)
        def _():
            rim_copy(0, 0, sent.at[:, lanes(0)]).wait_send()

        def finish(start, value):
            where = pl.ds(start, 32)
            target = pl.ds(pl.multiple_of(chan * channels + start, 32), 32)
            value = value * silu_slope(raw_first[plane, where, :])
            sent[where, lanes(plane)] = value
            full[target, lanes(plane + 1)] = value

        conv_sum(finish)
        pl.semaphore_wait(slot_sem.at[plane], chips)
        send_slot(1, plane + 1)

    other_copy(0).wait_recv()
    build_moved(1, other2)
    copy_near()
    slots_loop(when_far(gather_forward, 0))
    slots_loop(when_far(gather_finish, 0))
    slots_loop(split_far)
    for slot in (planes + 1, 0):
        when_exists(slot_sent, 0, 0)(slot)
    slots_loop(when_far(gather_sent, 0))
    tell(free_sem)

    @pl.loop(0, 6)
    def _(flow):
        weight_part(0, flow)

        @pl.when(flow == 0)
        def _():
            pl.semaphore_wait(free_sem, 1 + chips + rims)
            rim_start(1)
            for slot in range(1, planes + 1):
                send_pair(1, slot)

        @pl.when(flow == 2)
        def _():
            rim_spread(1)
            for slot in range(2, 4):
                gather_forward(1, 0, slot)

        @pl.when(flow == 3)
        def _():
            wide_event(0, 0)

        @pl.when(flow == 4)
        def _():
            for slot in range(1, planes + 1):
                far_start(1, 1, slot)
            for slot in (planes + 1, 0):
                when_far(far_start, 1)(slot)

    wide_event(0, 1)
    for slot in (*range(4, planes + 1), 1):
        gather_forward(1, 0, slot)
    build_moved(0, hidden)
    other_copy(1).wait_recv()
    wide_event(0, 2)
    build_moved(1, other1)
    for slot in (planes + 1, 0):
        when_exists(gather_forward, 1, 0)(slot)
    slots_loop(when_far(gather_forward, 1))
    slots_loop(when_exists(gather_finish, 1, 0))
    slots_loop(split_full)
    copy_near()
    slots_loop(when_far(gather_finish, 1))
    slots_loop(split_far)
    wide_event(0, 3)

    @pl.loop(0, 6)
    def _(flow):
        weight_part(1, flow)

        @pl.when((flow == 1) | (flow == 3))
        def _():
            wide_event(0, 4 + flow // 2)

        @pl.when(flow == 4)
        def _():
            wide_event(1, 0)

    split_taps(weight1_ref)
    wide_event(1, 1)
    for flow in range(5):
        deep_event(0, flow)

    @pl.loop(0, planes)
    def _(plane):
        conv_plane(plane)

        def finish(start, value):
            raw_out[plane, pl.ds(start, 32), :] = value

        conv_sum(finish)
        for index in range(min(planes, 6)):
            @pl.when(plane == index)
            def _():
                for layer, kind, flow in EVENTS[index]:
                    (wide_event, deep_event)[kind](layer, flow)

    result = pltpu.make_async_copy(raw_out, grad_ref, load_sem.at[0])
    result.start()
    for late in [*EVENTS[min(planes, 6) : 6], EVENTS[6]]:
        for layer, kind, flow in late:
            (wide_event, deep_event)[kind](layer, flow)
    result.wait()
    for flow in range(6):
        store_copy(1, flow).wait()
    slots_loop(when_exists(slot_sent, 1, 0))
    slots_loop(when_far(gather_sent, 1))
    rim_sent(1)
    other_copy(1).wait_send()
    for layer in range(2):
        for flow in range(6):
            wide_copy(layer, flow).wait_send()
            for j in range(1, members):
                deep_copy(layer, flow, j).wait_send()


def per_device(saved_input, pre_first, pre_second, out_grad, weight_first, weight_second):
    channels, planes, area = saved_input.shape
    total = weight_first.shape[2]
    slabs, chans = lax.axis_size("slab"), lax.axis_size("chan")
    side = math.isqrt(area)
    block = total // slabs
    groups = 128 // block
    steps = 9 * channels
    rows = steps // groups // 2
    width = planes * area
    wide = (planes + 2) * area
    chips, members, half = chans // 2, slabs // 4, total // 2
    dims = (slabs, chans, total, planes, area, side)
    hbm = pl.BlockSpec(memory_space=pl.ANY)
    cube = pltpu.VMEM((planes, channels, area), F32)
    flat = pltpu.VMEM((channels, width), F32)
    dma = pltpu.SemaphoreType.DMA
    out_part = jax.ShapeDtypeStruct((3, steps, block), F32)
    input_grad, first, second = pl.pallas_call(
        functools.partial(mega, dims),
        out_shape=(jax.ShapeDtypeStruct((planes, channels, area), F32), out_part, out_part),
        in_specs=[hbm] * 6,
        out_specs=(hbm, hbm, hbm),
        scratch_shapes=[
            *[cube] * 3,
            *[flat] * 4,
            pltpu.VMEM((total, wide), F32),
            pltpu.VMEM((half, wide), F32),
            *[pltpu.VMEM((total, wide), BF16)] * 2,
            *[pltpu.VMEM((2, half, wide), BF16)] * 2,
            *[pltpu.VMEM((2, steps, width), BF16)] * 2,
            *[pltpu.VMEM((3, steps, total), BF16)] * 2,
            pltpu.VMEM((2, steps // 2, total), F32),
            pltpu.VMEM((steps // 2, half), F32),
            pltpu.VMEM((steps, area), F32),
            *[pltpu.VMEM((6, 2, members, rows, 128), F32)] * 2,
            *[pltpu.VMEM((6, members, rows, 128), F32)] * 2,
            *[pltpu.VMEM((6, max(members - 1, 1), rows, 128), F32)] * 2,
            pltpu.VMEM((6, steps // 2, block), F32),
            dma((4,)),
            dma((2,)),
            *[dma((2, 2, planes + 2, 2 * chips))] * 2,
            *[dma((2, 2))] * 2,
            *[dma((2, planes + 2))] * 2,
            *[dma((2,))] * 2,
            *[dma((2, 6))] * 2,
            *[dma((2, 6, max(members - 1, 1)))] * 2,
            dma((2, 6)),
            pltpu.SemaphoreType.REGULAR,
            pltpu.SemaphoreType.REGULAR((planes,)),
        ],
        compiler_params=pltpu.CompilerParams(
            collective_id=0, has_side_effects=True, vmem_limit_bytes=67043328
        ),
        name="backward",
    )(
        *(value.transpose(1, 0, 2) for value in (saved_input, pre_first, pre_second, out_grad)),
        weight_first.reshape(3, steps, total),
        weight_second.reshape(3, steps, total),
    )
    scale = math.sqrt(planes * slabs * area)

    def finish(packed):
        return packed.reshape(27, channels, block) / scale

    return input_grad.transpose(1, 0, 2), finish(first), finish(second)


def solution(mesh):
    in_specs = (
        P("chan", "slab", None),
        P("chan", "slab", None),
        P("chan", "slab", None),
        P("chan", "slab", None),
        P(None, "chan", None),
        P(None, "chan", None),
    )
    out_specs = (P("chan", "slab", None), P(None, "chan", "slab"), P(None, "chan", "slab"))
    return jax.shard_map(
        per_device, mesh=mesh, in_specs=in_specs, out_specs=out_specs, check_vma=False
    )
```

time: 784 us -> 160 us (0.20)
  waiting for transfers between devices: 447 us -> 0 us
  local copies, waits for them, and re-layouts: 169 us -> 3.75 us
  Pallas kernels: 0 us -> 154 us
  matrix products: 99.9 us -> 0 us
  starting transfers between devices: 22.7 us -> 0 us
  other arithmetic: 25 us -> 2.32 us
  between operations: 15.2 us -> 0.65 us
    reduce_scatter x6 -> x0, waiting for transfers between devices: 426 us -> none  [reduce_parts(): lax.psum_scatter(part, 'slab', scatter_dimension=2, tiled=True)]
    pallas_call x0 -> x1, Pallas kernels: none -> 154 us  [per_device(): pl.pallas_call(functools.partial(mega, dims), out_shape=(jax.ShapeDtypeSt...]
    dot_general x8 -> x0, matrix products: 99.9 us -> none  [the longest x6 52.7 us: weight_side(): lax.dot_general(moved[1 + a:1 + a + planes], centre, (((0, 2), (0, 2)), (...]
    slice x30 -> x0, local copies, waits for them, and re-layouts: 87.8 us -> none  [the longest x8 77.2 us: weight_side(): moved[1 + a:1 + a + planes]]
    ppermute x8 -> x0, starting transfers between devices: 22.3 us -> none  [the longest x4 17.2 us: with_rim(): before = lax.ppermute(value[-1:], 'slab', up)]
    another operation x4 -> x0, local copies, waits for them, and re-layouts: 20.2 us -> none  [input_side(): near = jnp.stack([portion[1 - a:1 - a + planes] for a in STEPS], 0)]
    ppermute x8 -> x0, waiting for transfers between devices: 16.9 us -> none  [the longest x4 12.7 us: with_rim(): after = lax.ppermute(value[:1], 'slab', down)]
    unnamed x10 -> x0, other arithmetic: 13.8 us -> none
  transfers between devices with their start and end apart: 16 -> 0, of which waited for: 12 -> 0; matrix products, arithmetic and copies ran while one was open for 27% -> 0% of each run, Pallas kernels for 0% -> 0%
where the time goes in v2:
time: 160 us
  Pallas kernels  154 us (96%)
  local copies, waits for them, and re-layouts  3.75 us (2%)
  other arithmetic  2.32 us (1%)
    pallas_call x1, Pallas kernels, per_device(): pl.pallas_call(functools.partial(mega, dims), out_shape=(jax.ShapeDtypeSt...  154 us
    unnamed x5, local copies, waits for them, and re-layouts  3.75 us

profile of v2, /device:TPU:0, one launch (start us, length us, event | category | flops | bytes accessed | tf_op | source)
XLA Modules:
  0.0 160.2 jit_solution(1412395269576929216)
XLA Ops:
  0.6 153.5 %backward.1 = (f32[6,128,256]{2,1,0:T(8,128)}, f32[3,1152,64]{2,1,0:T(8,128)}, f32[3,1152,64]{2,1,0:T(8,128)}) custom-call(f32[6,128,256]{2,1,0:T(8,128)} %bitcast.13, f32[6,128,256]{2,1,0:T(8,128)} %bitcast.14, f32[6,128,256]{2,1,0:T(8,128)} %bitcast.15, f32[6,128,256]{2,1,0:T(8,128)} %bitcast.16, f32[3,1152,512]{2,1,0:T(8,128)} %bitcast.11, ...), custom_call_target="tpu_custom_call" | custom-call | tf_op jit(solution)/shard_map/backward/pallas_call | solution.py:767
  154.2 2.3 %broadcast_multiply_fusion = (f32[3,1152,64]{2,1,0:T(8,128)S(1)}, f32[3,1152,64]{2,1,0:T(8,128)S(1)}) fusion(f32[3,1152,64]{2,1,0:T(8,128)} %get-tuple-element.8, f32[3,1152,64]{2,1,0:T(8,128)} %get-tuple-element.7), kind=kLoop, calls=%fused_computation | loop fusion | flops 442368 | bytes 3538944 | tf_op jit(solution)/shard_map/div | solution.py:812
  156.5 1.4 copy.10
  157.9 0.0 copy-start
  157.9 1.4 copy.9
  159.4 0.0 copy-done
  159.4 0.9 copy.12
Async XLA Ops:
  157.9 1.4 copy-start

commit v3 on v2

--- a/solution.py
+++ b/solution.py
@@ -13,13 +13,13 @@
 MESH = pl.DeviceIdType.MESH
 STEPS = (-1, 0, 1)
 EVENTS = (
-    ((1, 0, 2), (0, 1, 5)),
-    ((1, 0, 3),),
+    ((1, 0, 3), (0, 1, 5)),
     ((1, 1, 0),),
-    ((1, 0, 4),),
-    ((1, 1, 1),),
-    ((1, 0, 5), (1, 1, 2)),
-    ((1, 1, 3), (1, 1, 4), (1, 1, 5)),
+    ((1, 0, 4), (1, 1, 1)),
+    ((1, 0, 5),),
+    ((1, 1, 2),),
+    ((1, 1, 3),),
+    ((1, 1, 4), (1, 1, 5)),
 )
 IN_PLANE = [(row_step, col_step) for row_step in STEPS for col_step in STEPS]
 
@@ -133,7 +133,6 @@
     signal(barrier, slab=beside)
     for j in range(1, members):
         signal(barrier, slab=deep_slab(j))
-    pl.semaphore_wait(barrier, 1 + members + chips + rims)
 
     def chan_rows(index):
         return pl.ds(pl.multiple_of(index * channels, channels), channels)
@@ -193,7 +192,7 @@
 
     def other_copy(layer):
         return pltpu.make_async_remote_copy(
-            src_ref=hidden,
+            src_ref=(hidden, raw_second)[layer],
             dst_ref=(other2, other1)[layer],
             send_sem=other_send.at[layer],
             recv_sem=other_recv.at[layer],
@@ -286,7 +285,7 @@
         def _():
             pair_copy(layer, slot, sent.at[:, lanes(slot - 1)]).start()
 
-    def rim_spread(layer):
+    def rim_take(layer):
         for toward in range(2):
             slot = (0, planes + 1)[toward]
 
@@ -294,11 +293,17 @@
             def _():
                 view = full.at[mine, lanes(slot)]
                 rim_copy(layer, toward, view).wait_recv()
-                gather_start(layer, 0, slot, view)
 
                 @pl.when(gives)
                 def _():
                     pair_copy(layer, slot, view).start()
+
+    def rim_spread(layer):
+        for slot in (planes + 1, 0):
+
+            @pl.when(exists(0, slot))
+            def _():
+                gather_start(layer, 0, slot, full.at[mine, lanes(slot)])
 
     def far_start(layer, kind, slot):
         @pl.when(takes)
@@ -337,14 +342,14 @@
                 full_h[where, lanes(slot)] = jnp.zeros((32, area), BF16)
                 full_l[where, lanes(slot)] = jnp.zeros((32, area), BF16)
 
-    def copy_near():
+    def copy_near(slot, count):
         @pl.loop(0, half // 32)
         def _(index):
             start = pl.multiple_of(index * 32, 32)
             group = start // owned
             where = pl.ds(pl.multiple_of(start + (group + parity) * owned, 32), 32)
-            near_h[0, pl.ds(start, 32), :] = full_h[where, :]
-            near_l[0, pl.ds(start, 32), :] = full_l[where, :]
+            near_h[0, pl.ds(start, 32), lanes(slot, count)] = full_h[where, lanes(slot, count)]
+            near_l[0, pl.ds(start, 32), lanes(slot, count)] = full_l[where, lanes(slot, count)]
 
     def split_far(slot):
         @pl.when(exists(1, slot))
@@ -380,13 +385,19 @@
         shift = (-(row_step * side + col_step)) % area
         return pltpu.roll(value, shift, 1) * mask_of(row_step, col_step)
 
+    def flat_rows(source):
+        return lambda plane, where: source[where, lanes(plane)]
+
+    def cube_rows(source):
+        return lambda plane, where: source[plane, where, :]
+
     def build_moved(piece, source):
         @pl.loop(0, planes)
         def _(plane):
             @pl.loop(0, channels // 32)
             def _(index):
                 start = pl.multiple_of(index * 32, 32)
-                value = source[pl.ds(start, 32), lanes(plane)]
+                value = source(plane, pl.ds(start, 32))
                 for tap, (row_step, col_step) in enumerate(IN_PLANE):
                     high, low = halves(shifted(value, row_step, col_step))
                     where = pl.ds(pl.multiple_of(tap * channels + start, 32), 32)
@@ -511,7 +522,6 @@
             value += dot_nt(moved_l[piece, where, :], near_h[piece, :, window])
         raw[...] = value
         pack(layer, flow)
-        wide_copy(layer, flow).start()
 
     def conv_plane(plane):
         value = jnp.zeros((steps, area), F32)
@@ -546,19 +556,20 @@
         sent[where, lanes(plane)] = raw_out[plane, where, :] * silu_slope(raw_second[plane, where, :])
 
     each_plane(make_sent)
+    load_copy(3).start()
+    load_copy(2).wait()
+
+    def make_hidden(plane, where):
+        value = raw_first[plane, where, :]
+        hidden[where, lanes(plane)] = value * jax.nn.sigmoid(value)
+
+    each_plane(make_hidden)
+    pl.semaphore_wait(barrier, 1 + members + chips + rims)
     rim_start(0)
     for slot in range(1, 4):
         send_slot(0, slot)
     for slot in range(1, planes + 1):
         send_pair(0, slot)
-    load_copy(3).start()
-    load_copy(2).wait()
-
-    def make_hidden(plane, where):
-        value = raw_first[plane, where, :]
-        hidden[where, lanes(plane)] = value * jax.nn.sigmoid(value)
-
-    each_plane(make_hidden)
 
     def keep_sent(plane, where):
         target = pl.ds(pl.multiple_of(chan * channels + where.start, 32), 32)
@@ -570,12 +581,11 @@
     stage_copy(weight1_ref, 1).start()
     for slot in range(4, planes + 1):
         send_slot(0, slot)
-    rim_spread(0)
-    build_moved(0, hidden)
+    rim_take(0)
     other_copy(0).start()
-    for slot in (1, 2):
+    build_moved(0, flat_rows(hidden))
+    for slot in (1, 2, 3):
         gather_forward(0, 0, slot)
-    gather_forward(0, 0, 3)
     for slot in (1, 2):
         gather_finish(0, 0, slot)
         split_full(slot)
@@ -583,44 +593,19 @@
     def when_far(action, layer):
         return when_exists(action, layer, 1)
 
-    def make_saved(plane, where):
-        hidden[where, lanes(plane)] = raw_second[plane, where, :]
-
-    @pl.loop(0, planes)
-    def _(index):
-        plane = (index + 1) % planes
-        slot = (index + 3) % (planes + 2)
-
-        @pl.when(exists(0, slot))
-        def _():
-            gather_finish(0, 0, slot)
-
-        split_full(slot)
+    def inner_slots(action):
+        @pl.loop(1, planes + 1)
+        def _(slot):
+            action(slot)
+
+    def conv_step(plane):
         slot_sent(0, 0, plane + 1)
         for j in range(1, chips):
             signal(slot_sem.at[plane], chan=far_chan(j))
         signal(slot_sem.at[plane], chan=partner)
         conv_plane(plane)
-        following = (index + 4) % (planes + 2)
-
-        @pl.when((index < planes - 1) & exists(0, following))
-        def _():
-            gather_forward(0, 0, following)
-
-        @pl.when(index == 0)
-        def _():
-            for late in range(1, planes + 1):
-                far_start(0, 1, late)
-            for late in (planes + 1, 0):
-                when_far(far_start, 0)(late)
-
-        @pl.when(index == planes - 2)
-        def _():
-            load_copy(3).wait()
-            other_copy(0).wait_send()
-            each_plane(make_saved)
-            other_copy(1).start()
-
+
+    def conv_finish(plane):
         @pl.when((plane == 0) & has_left)
         def _():
             rim_copy(0, 1, sent.at[:, lanes(0)]).wait_send()
@@ -637,79 +622,159 @@
             full[target, lanes(plane + 1)] = value
 
         conv_sum(finish)
+
+    def send_result(plane):
         pl.semaphore_wait(slot_sem.at[plane], chips)
         send_slot(1, plane + 1)
 
+    @pl.loop(0, planes - 2)
+    def _(index):
+        plane = index + 1
+        slot = index + 3
+        gather_finish(0, 0, slot)
+        split_full(slot)
+        conv_step(plane)
+
+        @pl.when(index < planes - 3)
+        def _():
+            gather_forward(0, 0, slot + 1)
+
+        @pl.when(index == 0)
+        def _():
+            for late in range(1, planes + 1):
+                far_start(0, 1, late)
+            rim_spread(0)
+
+        @pl.when(index == 2)
+        def _():
+            for late in (planes + 1, 0):
+                when_far(far_start, 0)(late)
+
+        conv_finish(plane)
+
+    inner_slots(functools.partial(gather_forward, 0, 1))
+    inner_slots(functools.partial(gather_finish, 0, 1))
+    inner_slots(split_far)
+    copy_near(1, planes)
     other_copy(0).wait_recv()
-    build_moved(1, other2)
-    copy_near()
-    slots_loop(when_far(gather_forward, 0))
-    slots_loop(when_far(gather_finish, 0))
-    slots_loop(split_far)
+    load_copy(3).wait()
+    other_copy(1).start()
+    build_moved(1, flat_rows(other2))
+
+    @pl.loop(1, planes - 1)
+    def _(plane):
+        send_result(plane)
+
+    def second_part(flow):
+        weight_part(0, flow)
+        wide_copy(0, flow).start()
+
+    @pl.loop(0, 2)
+    def _(flow):
+        second_part(flow)
+
+        @pl.when(flow == 0)
+        def _():
+            for slot in (planes + 1, 0):
+                when_exists(gather_forward, 0, 0)(slot)
+                when_far(gather_forward, 0)(slot)
+
+    for slot in (planes + 1, 0):
+        when_exists(gather_finish, 0, 0)(slot)
+        when_far(gather_finish, 0)(slot)
+        split_full(slot)
+        split_far(slot)
+        copy_near(slot, 1)
     for slot in (planes + 1, 0):
         when_exists(slot_sent, 0, 0)(slot)
     slots_loop(when_far(gather_sent, 0))
     tell(free_sem)
 
-    @pl.loop(0, 6)
+    @pl.loop(0, 2)
+    def _(index):
+        plane = (index + planes - 1) % planes
+        conv_step(plane)
+        conv_finish(plane)
+        send_result(plane)
+
+        @pl.when(index == 0)
+        def _():
+            pl.semaphore_wait(free_sem, 1 + chips + rims)
+            for slot in range(2, planes):
+                send_pair(1, slot)
+
+        send_pair(1, plane + 1)
+
+    rim_start(1)
+    wide_event(0, 0)
+
+    @pl.loop(2, 6)
     def _(flow):
-        weight_part(0, flow)
-
-        @pl.when(flow == 0)
-        def _():
-            pl.semaphore_wait(free_sem, 1 + chips + rims)
-            rim_start(1)
-            for slot in range(1, planes + 1):
-                send_pair(1, slot)
-
-        @pl.when(flow == 2)
-        def _():
-            rim_spread(1)
-            for slot in range(2, 4):
+        second_part(flow)
+
+        @pl.when(flow == 3)
+        def _():
+            wide_event(0, 1)
+
+            @pl.loop(2, planes)
+            def _(slot):
                 gather_forward(1, 0, slot)
 
-        @pl.when(flow == 3)
-        def _():
-            wide_event(0, 0)
-
         @pl.when(flow == 4)
         def _():
-            for slot in range(1, planes + 1):
+            for slot in (*range(2, planes + 1), 1):
                 far_start(1, 1, slot)
-            for slot in (planes + 1, 0):
-                when_far(far_start, 1)(slot)
-
-    wide_event(0, 1)
-    for slot in (*range(4, planes + 1), 1):
+
+    wide_event(0, 2)
+    build_moved(0, cube_rows(raw_second))
+    rim_take(1)
+    rim_spread(1)
+    wide_event(0, 3)
+    for slot in (planes, 1):
         gather_forward(1, 0, slot)
-    build_moved(0, hidden)
     other_copy(1).wait_recv()
-    wide_event(0, 2)
-    build_moved(1, other1)
+    build_moved(1, cube_rows(other1))
+    wide_event(0, 4)
     for slot in (planes + 1, 0):
-        when_exists(gather_forward, 1, 0)(slot)
-    slots_loop(when_far(gather_forward, 1))
-    slots_loop(when_exists(gather_finish, 1, 0))
-    slots_loop(split_full)
-    copy_near()
-    slots_loop(when_far(gather_finish, 1))
-    slots_loop(split_far)
-    wide_event(0, 3)
+        when_far(far_start, 1)(slot)
+    inner_slots(functools.partial(gather_forward, 1, 1))
+    inner_slots(functools.partial(gather_finish, 1, 0))
+    inner_slots(split_full)
+    copy_near(1, planes)
+    inner_slots(functools.partial(gather_finish, 1, 1))
+    inner_slots(split_far)
 
     @pl.loop(0, 6)
     def _(flow):
         weight_part(1, flow)
-
-        @pl.when((flow == 1) | (flow == 3))
-        def _():
-            wide_event(0, 4 + flow // 2)
-
-        @pl.when(flow == 4)
+        wide_copy(1, flow).start()
+
+        @pl.when(flow == 0)
+        def _():
+            wide_event(0, 5)
+            for slot in (planes + 1, 0):
+                when_exists(gather_forward, 1, 0)(slot)
+                when_far(gather_forward, 1)(slot)
+
+        @pl.when(flow == 1)
+        def _():
+            for slot in (planes + 1, 0):
+                when_exists(gather_finish, 1, 0)(slot)
+                when_far(gather_finish, 1)(slot)
+                split_full(slot)
+                split_far(slot)
+                copy_near(slot, 1)
+
+        @pl.when(flow == 3)
         def _():
             wide_event(1, 0)
 
+        @pl.when(flow == 5)
+        def _():
+            wide_event(1, 1)
+
     split_taps(weight1_ref)
-    wide_event(1, 1)
+    wide_event(1, 2)
     for flow in range(5):
         deep_event(0, flow)
 
@@ -738,8 +803,8 @@
     slots_loop(when_exists(slot_sent, 1, 0))
     slots_loop(when_far(gather_sent, 1))
     rim_sent(1)
-    other_copy(1).wait_send()
     for layer in range(2):
+        other_copy(layer).wait_send()
         for flow in range(6):
             wide_copy(layer, flow).wait_send()
             for j in range(1, members):
@@ -771,7 +836,8 @@
         out_specs=(hbm, hbm, hbm),
         scratch_shapes=[
             *[cube] * 3,
-            *[flat] * 4,
+            *[flat] * 3,
+            cube,
             pltpu.VMEM((total, wide), F32),
             pltpu.VMEM((half, wide), F32),
             *[pltpu.VMEM((total, wide), BF16)] * 2,
@@ -808,8 +874,8 @@
     )
     scale = math.sqrt(planes * slabs * area)
 
-    def finish(packed):
-        return packed.reshape(27, channels, block) / scale
+    def finish(summed):
+        return summed.reshape(27, channels, block) / scale
 
     return input_grad.transpose(1, 0, 2), finish(first), finish(second)
 

time: 160 us -> 152 us (0.950)
  Pallas kernels: 154 us -> 145 us
    pallas_call x1, Pallas kernels: 154 us -> 145 us  [per_device(): pl.pallas_call(functools.partial(mega, dims), out_shape=(jax.ShapeDtypeSt...]
where the time goes in v3:
time: 152 us
  Pallas kernels  145 us (95%)
  local copies, waits for them, and re-layouts  3.75 us (2%)
  other arithmetic  2.32 us (2%)
    pallas_call x1, Pallas kernels, per_device(): pl.pallas_call(functools.partial(mega, dims), out_shape=(jax.ShapeDtypeSt...  145 us
    unnamed x5, local copies, waits for them, and re-layouts  3.75 us

profile of v3, /device:TPU:0, one launch (start us, length us, event | category | flops | bytes accessed | tf_op | source)
XLA Modules:
  0.0 151.9 jit_solution(9171269320224390490)
XLA Ops:
  0.6 145.2 %backward.1 = (f32[6,128,256]{2,1,0:T(8,128)}, f32[3,1152,64]{2,1,0:T(8,128)}, f32[3,1152,64]{2,1,0:T(8,128)}) custom-call(f32[6,128,256]{2,1,0:T(8,128)} %bitcast.13, f32[6,128,256]{2,1,0:T(8,128)} %bitcast.14, f32[6,128,256]{2,1,0:T(8,128)} %bitcast.15, f32[6,128,256]{2,1,0:T(8,128)} %bitcast.16, f32[3,1152,512]{2,1,0:T(8,128)} %bitcast.11, ...), custom_call_target="tpu_custom_call" | custom-call | tf_op jit(solution)/shard_map/backward/pallas_call | solution.py:832
  145.8 2.3 %broadcast_multiply_fusion = (f32[3,1152,64]{2,1,0:T(8,128)S(1)}, f32[3,1152,64]{2,1,0:T(8,128)S(1)}) fusion(f32[3,1152,64]{2,1,0:T(8,128)} %get-tuple-element.8, f32[3,1152,64]{2,1,0:T(8,128)} %get-tuple-element.7), kind=kLoop, calls=%fused_computation | loop fusion | flops 442368 | bytes 3538944 | tf_op jit(solution)/shard_map/div | solution.py:878
  148.1 1.4 copy.10
  149.5 0.0 copy-start
  149.5 1.4 copy.9
  151.0 0.0 copy-done
  151.0 0.9 copy.12
Async XLA Ops:
  149.5 1.4 copy-start

commit v4 on v3

--- a/solution.py
+++ b/solution.py
@@ -875,7 +875,8 @@
     scale = math.sqrt(planes * slabs * area)
 
     def finish(summed):
-        return summed.reshape(27, channels, block) / scale
+        turned = lax.optimization_barrier(summed.reshape(27, channels, block).transpose(0, 2, 1))
+        return (turned / scale).transpose(0, 2, 1)
 
     return input_grad.transpose(1, 0, 2), finish(first), finish(second)
 

time: 152 us -> 152 us (level)
    reshape x0 -> x2, local copies, waits for them, and re-layouts: none -> 4.06 us  [finish(): summed.reshape(27, channels, block).transpose(0, 2, 1)]
    unnamed x5 -> x3, local copies, waits for them, and re-layouts: 3.75 us -> 0.88 us
    div x1 -> x0, other arithmetic: 2.32 us -> none  [finish(): return summed.reshape(27, channels, block) / scale]
where the time goes in v4:
time: 152 us
  Pallas kernels  145 us (95%)
  local copies, waits for them, and re-layouts  4.94 us (3%)
    pallas_call x1, Pallas kernels, per_device(): pl.pallas_call(functools.partial(mega, dims), out_shape=(jax.ShapeDtypeSt...  145 us
    reshape x2, local copies, waits for them, and re-layouts, finish(): summed.reshape(27, channels, block).transpose(0, 2, 1)  4.06 us

profile of v4, /device:TPU:0, one launch (start us, length us, event | category | flops | bytes accessed | tf_op | source)
XLA Modules:
  0.0 152.1 jit_solution(13403454146822605809)
XLA Ops:
  0.6 145.2 %backward.1 = (f32[6,128,256]{2,1,0:T(8,128)}, f32[3,1152,64]{2,1,0:T(8,128)}, f32[3,1152,64]{2,1,0:T(8,128)}) custom-call(f32[6,128,256]{2,1,0:T(8,128)} %bitcast.21, f32[6,128,256]{2,1,0:T(8,128)} %bitcast.22, f32[6,128,256]{2,1,0:T(8,128)} %bitcast.23, f32[6,128,256]{2,1,0:T(8,128)} %bitcast.24, f32[3,1152,512]{2,1,0:T(8,128)} %bitcast.15, ...), custom_call_target="tpu_custom_call" | custom-call | tf_op jit(solution)/shard_map/backward/pallas_call | solution.py:832
  145.8 0.0 copy-start
  145.8 2.1 %copy.9 = f32[27,128,64]{1,2,0:T(8,128)S(1)} copy(f32[27,128,64]{2,1,0:T(8,128)} %bitcast.20) | data formatting | bytes 1769472 | tf_op jit(solution)/shard_map/reshape | solution.py:878
  147.9 2.0 %copy.10 = f32[27,128,64]{1,2,0:T(8,128)S(1)} copy(f32[27,128,64]{2,1,0:T(8,128)} %bitcast.19) | data formatting | bytes 1769472 | tf_op jit(solution)/shard_map/reshape | solution.py:878
  149.9 1.4 multiply_bitcast_fusion
  151.2 0.0 copy-done
  151.2 0.9 copy.12
Async XLA Ops:
  145.8 5.5 %copy-start = (f32[6,128,256]{2,1,0:T(8,128)S(1)}, f32[6,128,256]{2,1,0:T(8,128)}, u32[]{:S(2)}) copy-start(f32[6,128,256]{2,1,0:T(8,128)} %get-tuple-element.6) | copy-start | bytes 2359300
